TPU v7x, 256 devices: a 4x2x16 block of a 4x16x16 slice. The times are simulated.
256 devices in a mesh: groups: 2 (over y), grid: 32 (over z, core), depth: 4 (over x).
Axes of the slice: x: 4, y: 2, z: 16, core: 2. Of those that a mesh axis runs over, the one named last changes fastest.
The devices are a block of a 4x16x16 slice.
Arguments:
- tokens: bfloat16 [4096, 4096], P(('groups', 'grid'), 'depth'), parts along dimension 0, may hold values from -6 to 6
- gate_weight: bfloat16 [4096, 14336], P('depth', 'grid'), may hold values from -0.09375 to 0.09375
- up_weight: bfloat16 [4096, 14336], P('depth', 'grid'), may hold values from -0.09375 to 0.09375
- down_weight: bfloat16 [14336, 4096], P('grid', 'depth'), may hold values from -0.046875 to 0.046875
Outputs:
- mixed: bfloat16 [4096, 4096], P(('groups', 'grid'), 'depth'), parts along dimension 0
There are 2 independent parts, one for each index of `groups`. A program takes and returns all parts, laid end to end along the dimension named above; an argument that names none is the same for every part. Nothing has to cross between parts.
All inputs are finite; a program needn't handle non-finite values.
Results may differ from a plain program's by a relative error of at most 0.0049.
Values may be sent and summed in bfloat16 or wider, within the bound.
A program may use at most 64 MiB of HBM per device.

v0:
```python
import jax
import jax.numpy as jnp
from jax import lax
from jax.sharding import Mesh
from jax.sharding import PartitionSpec as P

GRID = ("grid_0", "grid_1")
GROUPS_GRID = ("groups", "grid_0", "grid_1")


def joined_along(blocks, dim):
    shape = list(blocks.shape[1:])
    shape[dim] *= blocks.shape[0]
    return jnp.moveaxis(blocks, 0, dim).reshape(shape)


def sent_to_all(value, axis):
    copies = jnp.broadcast_to(value, (lax.axis_size(axis), *value.shape))
    return lax.all_to_all(copies, axis, split_axis=0, concat_axis=0, tiled=True)


def gathered_copies(value, axis, dim):
    return joined_along(sent_to_all(value, axis), dim)


def own_block(blocks, axes, sequence):
    shape = [lax.axis_size(a) for a in axes]
    blocks = blocks.reshape(*shape, *blocks.shape[1:])
    blocks = blocks.transpose(*sequence, *range(len(axes), blocks.ndim))
    blocks = blocks.reshape(-1, *blocks.shape[len(axes) :])
    for k in sequence:
        blocks = lax.psum_scatter(blocks, axes[k], scatter_dimension=0, tiled=True)
    return blocks[0]


def cut_along(value, dim, length):
    shape = value.shape
    blocks = value.reshape(*shape[:dim], length, shape[dim] // length, *shape[dim + 1 :])
    return jnp.moveaxis(blocks, dim, 0)


def scatter_axes(value, axes, sequence, dim):
    length = lax.axis_size(axes)
    return own_block(cut_along(value, dim, length), axes, sequence)


def body(tokens, gate_weight, up_weight, down_weight):
    grid_size = lax.axis_size(GRID)
    block_rows = tokens.shape[0]
    total_rows = block_rows * grid_size
    width_share = gate_weight.shape[1]
    stacked = jnp.concatenate([gate_weight, up_weight], axis=1)
    pre_act = jnp.dot(
        lax.all_gather(tokens, GRID, axis=0, tiled=True),
        stacked,
        preferred_element_type=jnp.float32,
    )
    blocked = pre_act.reshape(grid_size, block_rows, 2 * width_share)
    summed = lax.psum_scatter(blocked, "depth", scatter_dimension=1, tiled=True)
    hidden = gathered_copies(
        (jax.nn.silu(summed[..., :width_share]) * summed[..., width_share:]).astype(jnp.bfloat16),
        "depth",
        1,
    ).reshape(total_rows, width_share)
    return scatter_axes(
        jnp.dot(hidden, down_weight, preferred_element_type=jnp.float32), GRID, (1, 0), 0
    ).astype(jnp.bfloat16)


def solution(mesh):
    torus = Mesh(
        mesh.devices.reshape(mesh.shape["groups"], 16, 2, mesh.shape["depth"]),
        ("groups", "grid_0", "grid_1", "depth"),
    )
    placed = (P(GROUPS_GRID, "depth"), P("depth", GRID), P("depth", GRID), P(GRID, "depth"))
    return jax.shard_map(
        body, mesh=torus, in_specs=placed, out_specs=P(GROUPS_GRID, "depth"), check_vma=False
    )
```

profile of v0, /device:TPU:40, one launch (start us, length us, event | category | flops | bytes accessed | tf_op | source)
XLA Modules:
  0.0 342.8 jit_solution(1183751066836995780)
XLA Ops:
  6.5 0.0 copy-start
  6.6 0.0 all-gather.2.cloned.1.call-start
  6.6 0.7 all-gather.2.cloned.1.call-update
  7.3 0.1 reduce-scatter.4.cloned.1.call-start
  7.4 86.7 %all-gather.2.cloned.1.call-done = bf16[2048,1024]{1,0:T(8,128)(2,1)} async-done(((bf16[64,1024]{1,0:T(8,128)(2,1)}), bf16[2048,1024]{1,0:T(8,128)(2,1)}) %all-gather.2.cloned.1.call-update) | async-done | bytes 4194320 | tf_op jit(solution)/shard_map/all_gather | solution.py:54
  94.1 9.7 %convolution_bitcast_fusion = f32[2048,896]{0,1:T(8,128)} fusion(bf16[2048,1024]{1,0:T(8,128)(2,1)} %all-gather.2.cloned.1.call-done, bf16[1024,448]{0,1:T(8,128)(2,1)} %param.6, bf16[1024,448]{0,1:T(8,128)(2,1)} %param.5), kind=kOutput, calls=%fused_computation | convolution fusion | flops 3761766400 | bytes 13369344 | tf_op jit(solution)/shard_map/dot_general | solution.py:53
  103.8 8.6 %copy.8 = f32[2048,896]{1,0:T(8,128)} copy(f32[2048,896]{0,1:T(8,128)} %convolution_bitcast_fusion) | data formatting | bytes 14680064 | tf_op jit(solution)/shard_map/dot_general | solution.py:53
  112.4 0.1 reduce-scatter.4.cloned.1.call-update
  112.4 0.1 reduce-scatter.6.cloned.1.call-start
  112.5 76.0 %reduce-scatter.4.cloned.1.call-done = f32[32,16,896]{2,1,0:T(8,128)} async-done(((f32[32,64,896]{2,1,0:T(8,128)}), f32[32,16,896]{2,1,0:T(8,128)}) %reduce-scatter.4.cloned.1.call-update) | async-done | bytes 1835024 | tf_op jit(solution)/shard_map/reduce_scatter | solution.py:59
  188.5 1.9 fusion.3
  190.5 0.3 broadcast_in_dim.3
  190.7 29.1 %all_to_all.5 = bf16[4,32,16,448]{3,2,1,0:T(8,128)(2,1)S(1)} all-to-all(bf16[4,32,16,448]{3,2,1,0:T(8,128)(2,1)S(1)} %broadcast_in_dim.3), channel_id=1, replica_groups=mesh['groups'=2,'grid_0'=16,'grid_1'=2,'depth'=4] {'depth'}, dimensions={0} | all-to-all | bytes 3670016 | tf_op jit(solution)/shard_map/all_to_all | solution.py:19
  219.8 0.2 copy.9
  220.0 0.0 copy-done
  220.0 2.3 convolution_bitcast_fusion.1
  222.4 4.1 %copy.10 = f32[2,16,64,1024]{3,2,1,0:T(8,128)} copy(f32[2,16,64,1024]{3,2,0,1:T(8,128)S(1)} %convolution_bitcast_fusion.1) | data formatting | bytes 16777216 | tf_op jit(solution)/shard_map/transpose | solution.py:29
  226.5 0.1 reduce-scatter.6.cloned.1.call-update
  226.5 0.1 reduce-scatter.8.cloned.1.call-start
  226.6 24.9 %reduce-scatter.6.cloned.1.call-done = f32[16,64,1024]{2,1,0:T(8,128)} async-done(((f32[32,64,1024]{2,1,0:T(8,128)}), f32[16,64,1024]{2,1,0:T(8,128)}) %reduce-scatter.6.cloned.1.call-update) | async-done | bytes 4194320 | tf_op jit(solution)/shard_map/reduce_scatter | solution.py:32
  251.5 0.1 reduce-scatter.8.cloned.1.call-update
  251.6 83.0 %reduce-scatter.8.cloned.1.call-done = f32[1,64,1024]{2,1,0:T(8,128)} async-done(((f32[16,64,1024]{2,1,0:T(8,128)}), f32[1,64,1024]{2,1,0:T(8,128)}) %reduce-scatter.8.cloned.1.call-update) | async-done | bytes 262160 | tf_op jit(solution)/shard_map/reduce_scatter | solution.py:32
  334.6 1.6 convert_bitcast_fusion
Async XLA Ops:
  6.5 213.5 %copy-start = (bf16[448,1024]{1,0:T(8,128)(2,1)S(1)}, bf16[448,1024]{1,0:T(8,128)(2,1)}, u32[]{:S(2)}) copy-start(bf16[448,1024]{1,0:T(8,128)(2,1)} %param.7) | copy-start | bytes 2752516
  6.6 87.5 %all-gather.2.cloned.1.call-start = ((), (), s32[]{:S(2)}) async-start(), calls=%async_computation.4 | async-start | bytes 4325376 | tf_op jit(solution)/shard_map/all_gather | solution.py:54
  7.3 181.2 %reduce-scatter.4.cloned.1.call-start = ((), (), s32[]{:S(2)}) async-start(), calls=%async_computation.5 | async-start | bytes 9175040 | tf_op jit(solution)/shard_map/reduce_scatter | solution.py:59
  112.4 139.1 %reduce-scatter.6.cloned.1.call-start = ((), (), s32[]{:S(2)}) async-start(), calls=%async_computation.6 | async-start | bytes 12582912 | tf_op jit(solution)/shard_map/reduce_scatter | solution.py:32
  226.5 108.1 %reduce-scatter.8.cloned.1.call-start = ((), (), s32[]{:S(2)}) async-start(), calls=%async_computation.7 | async-start | bytes 4456448 | tf_op jit(solution)/shard_map/reduce_scatter | solution.py:32
Sparse Core Ops, SparseCore 0:
  9.2 84.8 all-gather.1
  112.6 75.8 reduce-scatter.3
  226.6 24.8 reduce-scatter.5
  254.0 80.6 reduce-scatter.7
where the time goes:
time: 343 us
  waiting for transfers between devices  272 us (79%)
  blocking collectives  29.1 us (8%)
  between operations  13.2 us (4%)
  local copies, waits for them, and re-layouts  13.1 us (4%)
  matrix products  12 us (3%)
  other arithmetic  3.57 us (1%)
    reduce_scatter x2, waiting for transfers between devices, own_block(): blocks = lax.psum_scatter(blocks, axes[k], scatter_dimension=0, tiled=True)  108 us
    all_gather x1, waiting for transfers between devices, body(): lax.all_gather(tokens, GRID, axis=0, tiled=True)  86.7 us
    reduce_scatter x1, waiting for transfers between devices, body(): summed = lax.psum_scatter(blocked, 'depth', scatter_dimension=1, tiled=True)  76 us
    all_to_all x1, blocking collectives, sent_to_all(): return lax.all_to_all(copies, axis, split_axis=0, concat_axis=0, tiled=True)  29.1 us
    dot_general x1, matrix products, body(): jnp.dot(lax.all_gather(tokens, GRID, axis=0, tiled=True), stacked, prefer...  9.69 us
    dot_general x1, local copies, waits for them, and re-layouts, body(): jnp.dot(lax.all_gather(tokens, GRID, axis=0, tiled=True), stacked, prefer...  8.59 us
  transfers between devices with their start and end apart: 4, of which 4 were waited for; matrix products, arithmetic and copies ran while one was open for 0% of the time, Pallas kernels for 0%

commit v1 on v0

v1 whole, which is shorter than its diff:
```python
import functools

import jax
import jax.numpy as jnp
from jax import lax
from jax.experimental import pallas as pl
from jax.experimental.pallas import tpu as pltpu
from jax.sharding import PartitionSpec as P

F32 = jnp.float32
BF16 = jnp.bfloat16

A_PIECES = 4
D_PIECES = 2
WIDE_HOPS = 3
LAG = 3


class Plan:
    def __init__(self, chips, block):
        self.S = chips // 2
        self.block = block
        self.total = block * chips

    def off(self, s):
        return 0 if s == 0 else self.block * (2 * s - 1)

    def rows(self, s):
        return self.block if s in (0, self.S) else 2 * self.block

    def order(self):
        half = self.S // 2
        return list(range(half)) + list(range(self.S, half - 1, -1))

    def pieces(self, s, way, n):
        if s < self.S:
            return list(range(n))
        return list(range(n // 2)) if way == 0 else list(range(n // 2, n))

    def ops(self):
        S, out = self.S, []
        za, zd = 2.8 / A_PIECES, 2.8 / D_PIECES
        out.append((("A", 0, 0), [], [], [(("a", 1, p), "z", za) for p in range(A_PIECES)], 0.1, 0))
        for s in range(1, S + 1):
            for p in range(A_PIECES):
                send = [(("a", s + 1, p), "z", za if s + 1 < S else za / 2)] if s < S else []
                out.append((("A", s, p), [("A", 0, 0)], [("a", s, p)], send, 0.06, 0))
        seq = self.order()
        for i, s in enumerate(seq):
            u = self.rows(s) / (2 * self.block)
            deps = [("A", s, p) for p in range(A_PIECES)] if s else [("A", 0, 0)]
            if i:
                deps.append(("M", seq[i - 1]))
            if i >= LAG:
                deps.append(("S", seq[i - LAG]))
            x = 1.23 * u
            out.append((("M", s), deps, [], [(("r", s), "x", x), (("d", s), "x", x)], 0.4 + 1.2 * u, 6))
            out.append((("R", s), [("M", s)], [("r", s)], [(("e", s), "x", x)], 0.15, 1))
            out.append((("S", s), [("R", s)], [("d", s), ("e", s)], [(("h", s), "x", x)], 0.3, 2))
            out.append((("F", s), [("S", s)], [("h", s)], [(("f", s), "x", x / 2)], 0.05, 1))
            out.append((("N", s), [("F", s)], [("f", s)], [], 0.3 + 0.5 * u, 5))
        for s in range(S, -1, -1):
            for p in range(D_PIECES):
                deps = [("N", s)]
                if s < S:
                    deps += [("Z", s + 1, q) for q in range(D_PIECES)]
                wait = [("z", s, p)] if s < S else []
                wide = 2 if s <= WIDE_HOPS else 1
                send = [(("z", s - 1, p), "z", wide * (zd if s < S else zd / 2))] if s else []
                out.append((("Z", s, p), deps, wait, send, 0.15, 4))
        return out

    def schedule(self, latency=2.2, start=3.5):
        ops = self.ops()
        done, arrives, free = set(), {}, {"x": 0.0, "z": 0.0}
        now, result = 0.0, []
        while ops:
            best = None
            for k, (name, deps, wait, send, cost, rank) in enumerate(ops):
                if any(d not in done for d in deps) or any(m not in arrives for m in wait):
                    continue
                ready = max([now] + [arrives[m] for m in wait])
                if name[0] == "M":
                    ready = max(ready, start)
                key = (ready, rank, k)
                if best is None or key < best[0]:
                    best = (key, k)
            name, deps, wait, send, cost, rank = ops.pop(best[1])
            now = best[0][0] + cost
            for message, link, length in send:
                free[link] = max(free[link], now) + length
                arrives[message] = free[link] + latency
            done.add(name)
            result.append((name, round(now, 2)))
        return result


def kernel(plan, tok, wg, wu, wd, out, X, W, WD, GV, UV, PB, SR, RR, SD, RD, H, O, ZS, ZR, YS, YR,
           local_sem, send_sem, recv_sem):
    S, B = plan.S, plan.block
    ring = 2 * 2 * S
    width = wg.shape[1]
    grid, me = lax.axis_index("grid"), lax.axis_index("depth")
    core = lax.rem(grid, 2)
    other = 1 - core
    partner = {"grid": grid + 1 - 2 * core}
    zway = ({"grid": lax.rem(grid + 2, ring)}, {"grid": lax.rem(grid + ring - 2, ring)})
    xway = ({"depth": lax.rem(me + 1, 4)}, {"depth": lax.rem(me + 3, 4)})

    numbers, started = {}, []

    def message(key, src, dst, to):
        n = numbers.setdefault(key, len(numbers))
        return pltpu.make_async_remote_copy(
            src_ref=src, dst_ref=dst, send_sem=send_sem.at[n], recv_sem=recv_sem.at[n],
            device_id=to, device_id_type=pl.DeviceIdType.MESH)

    def send(key, src, dst, to):
        m = message(key, src, dst, to)
        m.start()
        started.append(m)

    def arrived(key, dst, to):
        message(key, dst, dst, to).wait_recv()

    loads = [
        pltpu.make_async_copy(tok, X.at[pl.ds(0, B)], local_sem.at[0]),
        pltpu.make_async_copy(wg, GV, local_sem.at[1]),
        pltpu.make_async_copy(wu, UV, local_sem.at[2]),
        pltpu.make_async_copy(wd, WD.at[core], local_sem.at[3]),
    ]
    for load in loads:
        load.start()

    barrier = pltpu.get_barrier_semaphore()
    for to in (*zway, *xway, partner):
        pl.semaphore_signal(barrier, inc=1, device_id=to, device_id_type=pl.DeviceIdType.MESH)
    pl.semaphore_wait(barrier, 5)

    def a_rows(s, way, p):
        size = B // A_PIECES
        base = plan.off(s) + (B if way == 1 and 0 < s < S else 0)
        return pl.ds(base + p * size, size)

    def a_send(s, p):
        for way in (0, 1):
            if p in plan.pieces(s + 1, way, A_PIECES):
                send(("a", s + 1, way, p), X.at[a_rows(s, way, p)], X.at[a_rows(s + 1, way, p)], zway[way])

    def op_a(s, p=None):
        if s == 0:
            loads[0].wait()
            for p in range(A_PIECES):
                a_send(0, p)
            for load in loads[1:3]:
                load.wait()

            @pl.loop(0, wg.shape[0] // 128)
            def _(i):
                r = pl.ds(pl.multiple_of(i * 128, 128), 128)
                W[core, r, :] = jnp.concatenate([GV[r, :], UV[r, :]], axis=1)

            send(("w",), W.at[core], W.at[core], partner)
            loads[3].wait()
            send(("v",), WD.at[core], WD.at[core], partner)
            return
        for way in (0, 1):
            if p in plan.pieces(s, way, A_PIECES):
                dst = X.at[a_rows(s, way, p)]
                arrived(("a", s, way, p), dst, zway[way])
        if s < S:
            a_send(s, p)

    def quarter(s, k):
        size = plan.rows(s) // 4
        return pl.ds(pl.multiple_of(plan.off(s) + lax.rem(me + k, 4) * size, 16), size)

    def packed(s):
        return pl.ds(plan.off(s) // 4, plan.rows(s) // 4)

    def op_m(s):
        if s == 0:
            arrived(("w",), W.at[other], partner)
        r, q = pl.ds(plan.off(s), plan.rows(s)), packed(s)
        for half in (0, 1):
            PB[half, r, :] = jnp.dot(X[r, :], W[half], preferred_element_type=F32)
            SR[half, q, :] = PB[half, quarter(s, 2), :].astype(BF16)
            send(("r", s, half), SR.at[half, q], RR.at[half, q], xway[half])
        for way in (0, 1):
            half = 1 - way
            SD[way, half, q, :] = PB[half, quarter(s, 1 + 2 * way), :].astype(BF16)
            send(("d", s, way, half), SD.at[way, half, q], RD.at[way, half, q], xway[way])

    def op_r(s):
        q = packed(s)
        for way in (0, 1):
            arrived(("r", s, way), RR.at[way, q], xway[way])
            SD[way, way, q, :] = (PB[way, quarter(s, 1 + 2 * way), :] + RR[way, q, :].astype(F32)).astype(BF16)
            send(("d", s, way, way), SD.at[way, way, q], RD.at[way, way, q], xway[way])

    def op_s(s):
        q, mine = packed(s), quarter(s, 0)
        parts = []
        for way in (0, 1):
            for half in (0, 1):
                arrived(("d", s, way, half), RD.at[way, half, q], xway[way])
        for half in (0, 1):
            t = PB[half, mine, :] + RD[0, half, q, :].astype(F32) + RD[1, half, q, :].astype(F32)
            gate, up = t[:, :width], t[:, width:]
            parts.append(gate / (1.0 + jnp.exp(-gate)) * up)
        H[mine, :] = jnp.concatenate(parts, axis=1).astype(BF16)
        for way in (0, 1):
            send(("h", s, way), H.at[mine], H.at[mine], xway[way])

    def passed_on(s, way, k):
        size = plan.rows(s) // 4
        if s in (0, S):
            return quarter(s, k) if way == (0 if s == 0 else 1) else None
        start = plan.off(s) + lax.rem(me + k, 4) * size + way * (size // 2)
        return pl.ds(pl.multiple_of(start, 16), size // 2)

    def op_f(s):
        for way in (0, 1):
            k = 3 - 2 * way
            arrived(("h", s, way), H.at[quarter(s, k)], xway[way])
            part = passed_on(s, way, k)
            if part is not None:
                send(("f", s, way), H.at[part], H.at[part], xway[way])

    def op_n(s):
        if s == plan.order()[0]:
            arrived(("v",), WD.at[other], partner)
        for way in (0, 1):
            part = passed_on(s, way, 2)
            if part is not None:
                arrived(("f", s, way), H.at[part], xway[way])
        r = pl.ds(plan.off(s), plan.rows(s))
        depth = WD.shape[0] * WD.shape[1]
        O[r, :] = jnp.dot(H[r, :], WD[...].reshape(depth, WD.shape[2]), preferred_element_type=F32)

    def z_place(s, way, p):
        size = B // D_PIECES
        r = pl.ds(s * B + p * size, size)
        return (YS.at[way, r], YR.at[way, r]) if s < WIDE_HOPS else (ZS.at[way, r], ZR.at[way, r])

    def op_z(s, p):
        size = B // D_PIECES
        total = None
        for way in (0, 1):
            if p not in plan.pieces(s, way, D_PIECES):
                continue
            if s == 0:
                base = 0
            else:
                base = plan.off(s) + (B if way == 0 and s < S else 0)
            if total is None or s > 0:
                total = O[pl.ds(base + p * size, size), :]
            if s < S and p in plan.pieces(s + 1, way, D_PIECES):
                got = z_place(s, way, p)[1]
                arrived(("z", s, way, p), got, zway[way])
                total = total + got[...].astype(F32)
            if s > 0:
                src, dst = z_place(s - 1, way, p)
                src[...] = total.astype(src.dtype)
                send(("z", s - 1, way, p), src, dst, zway[way])
        if s == 0:
            out[pl.ds(p * size, size), :] = total.astype(BF16)

    run = {"A": op_a, "M": op_m, "R": op_r, "S": op_s, "F": op_f, "N": op_n, "Z": op_z}
    for (name, *at), _ in plan.schedule():
        run[name](*at)
    for m in started:
        m.wait_send()


def messages(plan):
    S = plan.S
    a = 2 * ((S - 1) * A_PIECES + A_PIECES // 2)
    z = 2 * ((S - 1) * D_PIECES + D_PIECES // 2)
    return a + z + 2 + (S + 1) * 8 + 2 * (S - 1) + 2


def body(tokens, gate_weight, up_weight, down_weight):
    block, deep = tokens.shape
    width, cols = down_weight.shape
    chips = lax.axis_size("grid") // 2
    plan = Plan(chips, block)
    total, quarters = plan.total, plan.total // 4
    vmem, any_ = pl.BlockSpec(memory_space=pltpu.VMEM), pl.BlockSpec(memory_space=pl.ANY)
    n = messages(plan)
    return pl.pallas_call(
        functools.partial(kernel, plan),
        out_shape=jax.ShapeDtypeStruct((block, cols), BF16),
        in_specs=[any_] * 4,
        out_specs=vmem,
        scratch_shapes=[
            pltpu.VMEM((total, deep), BF16),
            pltpu.VMEM((2, deep, 2 * width), BF16),
            pltpu.VMEM((2, width, cols), BF16),
            pltpu.VMEM((deep, width), BF16),
            pltpu.VMEM((deep, width), BF16),
            pltpu.VMEM((2, total, 2 * width), F32),
            pltpu.VMEM((2, quarters, 2 * width), BF16),
            pltpu.VMEM((2, quarters, 2 * width), BF16),
            pltpu.VMEM((2, 2, quarters, 2 * width), BF16),
            pltpu.VMEM((2, 2, quarters, 2 * width), BF16),
            pltpu.VMEM((total, 2 * width), BF16),
            pltpu.VMEM((total, cols), F32),
            pltpu.VMEM((2, total // 2, cols), BF16),
            pltpu.VMEM((2, total // 2, cols), BF16),
            pltpu.VMEM((2, max(1, WIDE_HOPS) * block, cols), F32),
            pltpu.VMEM((2, max(1, WIDE_HOPS) * block, cols), F32),
            pltpu.SemaphoreType.DMA((4,)),
            pltpu.SemaphoreType.DMA((n,)),
            pltpu.SemaphoreType.DMA((n,)),
        ],
        compiler_params=pltpu.CompilerParams(
            collective_id=0, has_side_effects=True, vmem_limit_bytes=60 * 1024 * 1024),
    )(tokens, gate_weight, up_weight, down_weight)


def solution(mesh):
    return jax.shard_map(
        body,
        mesh=mesh,
        in_specs=(P(("groups", "grid"), "depth"), P("depth", "grid"), P("depth", "grid"), P("grid", "depth")),
        out_specs=P(("groups", "grid"), "depth"),
        check_vma=False,
    )
```

time: 343 us -> 121 us (0.35)
  waiting for transfers between devices: 272 us -> 0 us
  Pallas kernels: 0 us -> 116 us
  blocking collectives: 29.1 us -> 0 us
  between operations: 13.2 us -> 0.01 us
  matrix products: 12 us -> 0 us
  local copies, waits for them, and re-layouts: 13.1 us -> 5.22 us
  other arithmetic: 3.57 us -> 0 us
    reduce_scatter x3 -> x0, waiting for transfers between devices: 184 us -> none  [the longest x2 108 us: own_block(): blocks = lax.psum_scatter(blocks, axes[k], scatter_dimension=0, tiled=True)]
    pallas_call x0 -> x1, Pallas kernels: none -> 116 us  [body(): pl.pallas_call(functools.partial(kernel, plan), out_shape=jax.ShapeDtypeS...]
    all_gather x1 -> x0, waiting for transfers between devices: 86.7 us -> none  [body(): lax.all_gather(tokens, GRID, axis=0, tiled=True)]
    all_to_all x1 -> x0, blocking collectives: 29.1 us -> none  [sent_to_all(): return lax.all_to_all(copies, axis, split_axis=0, concat_axis=0, tiled=True)]
    dot_general x2 -> x0, matrix products: 12 us -> none  [the longest x1 9.69 us: body(): jnp.dot(lax.all_gather(tokens, GRID, axis=0, tiled=True), stacked, prefer...]
    dot_general x1 -> x0, local copies, waits for them, and re-layouts: 8.59 us -> none  [body(): jnp.dot(lax.all_gather(tokens, GRID, axis=0, tiled=True), stacked, prefer...]
    unnamed x2 -> x5, local copies, waits for them, and re-layouts: 0.01 us -> 5.22 us
    transpose x2 -> x0, local copies, waits for them, and re-layouts: 4.3 us -> none  [the longest x1 4.06 us: own_block(): blocks = blocks.transpose(*sequence, *range(len(axes), blocks.ndim))]
  transfers between devices with their start and end apart: 4 -> 0, of which waited for: 4 -> 0; matrix products, arithmetic and copies ran while one was open for 0% -> 0% of each run, Pallas kernels for 0% -> 0%
where the time goes in v1:
time: 121 us
  Pallas kernels  116 us (96%)
  local copies, waits for them, and re-layouts  5.22 us (4%)
    pallas_call x1, Pallas kernels, body(): pl.pallas_call(functools.partial(kernel, plan), out_shape=jax.ShapeDtypeS...  116 us
    unnamed x5, local copies, waits for them, and re-layouts  5.22 us

profile of v1, /device:TPU:40, one launch (start us, length us, event | category | flops | bytes accessed | tf_op | source)
XLA Modules:
  0.0 121.2 jit_solution(9595533558222906914)
XLA Ops:
  0.0 0.0 copy-start
  0.0 2.3 %copy.5.wg = bf16[1024,448]{1,0:T(8,128)(2,1)} copy(bf16[1024,448]{0,1:T(8,128)(2,1)} %param.5) | data formatting | bytes 1835008 | tf_op args[1]
  2.3 0.0 copy-done
  2.3 1.3 %copy.6.wu = bf16[1024,448]{1,0:T(8,128)(2,1)} copy(bf16[1024,448]{0,1:T(8,128)(2,1)S(1)} %copy-done) | data formatting | bytes 1835008 | tf_op args[2]
  3.7 115.9 %shard_map.46 = bf16[64,1024]{1,0:T(8,128)(2,1)} custom-call(bf16[64,1024]{1,0:T(8,128)(2,1)} %tok.1, bf16[1024,448]{1,0:T(8,128)(2,1)} %copy.5.wg, bf16[1024,448]{1,0:T(8,128)(2,1)} %copy.6.wu, bf16[448,1024]{1,0:T(8,128)(2,1)} %wd.1), custom_call_target="tpu_custom_call" | custom-call | tf_op jit(solution)/shard_map/pallas_call | solution.py:291
  119.6 1.6 %copy.8 = bf16[64,1024]{1,0:T(8,128)(2,1)} copy(bf16[64,1024]{1,0:T(8,128)(2,1)} %shard_map.46) | data formatting | bytes 262144
Async XLA Ops:
  0.0 2.3 %copy-start = (bf16[1024,448]{0,1:T(8,128)(2,1)S(1)}, bf16[1024,448]{0,1:T(8,128)(2,1)}, u32[]{:S(2)}) copy-start(bf16[1024,448]{0,1:T(8,128)(2,1)} %param.6) | copy-start | bytes 2752516

commit v2 on v1

--- a/solution.py
+++ b/solution.py
@@ -10,10 +10,16 @@
 F32 = jnp.float32
 BF16 = jnp.bfloat16
 
-A_PIECES = 4
-D_PIECES = 2
+A_ROWS = 4
+A_COLS = 2
+A_PIECES = A_ROWS * A_COLS
+D_PIECES = 4
 WIDE_HOPS = 3
-LAG = 3
+GATES = (("M", 1), ("R", 2))
+EARLY = 5
+DIRECT = 1
+SPLIT = False
+RANK = {"A": 0, "M": 6, "D": 5, "R": 1, "S": 2, "F": 1, "N": 5, "Z": 4}
 
 
 class Plan:
@@ -28,9 +34,12 @@
     def rows(self, s):
         return self.block if s in (0, self.S) else 2 * self.block
 
+    def direct(self, s):
+        return s > self.S - DIRECT
+
     def order(self):
-        half = self.S // 2
-        return list(range(half)) + list(range(self.S, half - 1, -1))
+        early = min(EARLY, self.S)
+        return list(range(early)) + list(range(self.S, early - 1, -1))
 
     def pieces(self, s, way, n):
         if s < self.S:
@@ -40,37 +49,44 @@
     def ops(self):
         S, out = self.S, []
         za, zd = 2.8 / A_PIECES, 2.8 / D_PIECES
-        out.append((("A", 0, 0), [], [], [(("a", 1, p), "z", za) for p in range(A_PIECES)], 0.1, 0))
+        out.append((("A", 0, 0), [], [], [(("a", 1, p), "z", za) for p in range(A_PIECES)], 1.0, RANK["A"]))
         for s in range(1, S + 1):
             for p in range(A_PIECES):
                 send = [(("a", s + 1, p), "z", za if s + 1 < S else za / 2)] if s < S else []
-                out.append((("A", s, p), [("A", 0, 0)], [("a", s, p)], send, 0.06, 0))
+                out.append((("A", s, p), [("A", 0, 0)], [("a", s, p)], send, 0.04, RANK["A"]))
         seq = self.order()
         for i, s in enumerate(seq):
             u = self.rows(s) / (2 * self.block)
             deps = [("A", s, p) for p in range(A_PIECES)] if s else [("A", 0, 0)]
             if i:
                 deps.append(("M", seq[i - 1]))
-            if i >= LAG:
-                deps.append(("S", seq[i - LAG]))
+            stage, lag = GATES[i > EARLY]
+            if i >= lag and not (stage == "R" and self.direct(seq[i - lag])):
+                deps.append((stage, seq[i - lag]))
             x = 1.23 * u
-            out.append((("M", s), deps, [], [(("r", s), "x", x), (("d", s), "x", x)], 0.4 + 1.2 * u, 6))
-            out.append((("R", s), [("M", s)], [("r", s)], [(("e", s), "x", x)], 0.15, 1))
-            out.append((("S", s), [("R", s)], [("d", s), ("e", s)], [(("h", s), "x", x)], 0.3, 2))
-            out.append((("F", s), [("S", s)], [("h", s)], [(("f", s), "x", x / 2)], 0.05, 1))
-            out.append((("N", s), [("F", s)], [("f", s)], [], 0.3 + 0.5 * u, 5))
+            if self.direct(s):
+                out.append((("M", s), deps, [], [(("r", s), "x", 2 * x), (("d", s), "x", 2 * x)], 1.0, RANK["M"]))
+                out.append((("S", s), [("M", s)], [("r", s), ("d", s)], [(("h", s), "x", 2 * x)], 0.2, RANK["S"]))
+                out.append((("N", s), [("S", s)], [("h", s)], [], 0.45, RANK["N"]))
+                continue
+            if SPLIT:
+                out.append((("M", s), deps, [], [(("r", s), "x", x)], 1.0, RANK["M"]))
+                out.append((("D", s), [("M", s)], [], [(("d", s), "x", x)], 0.03, RANK["D"]))
+            else:
+                out.append((("M", s), deps, [], [(("r", s), "x", x), (("d", s), "x", x)], 1.0, RANK["M"]))
+            out.append((("R", s), [("M", s)], [("r", s)], [(("e", s), "x", x)], 0.05, RANK["R"]))
+            out.append((("S", s), [("R", s)] + [("D", s)] * SPLIT, [("d", s), ("e", s)], [(("h", s), "x", x)], 0.2, RANK["S"]))
+            out.append((("F", s), [("S", s)], [("h", s)], [(("f", s), "x", x / 2)], 0.02, RANK["F"]))
+            out.append((("N", s), [("F", s)], [("f", s)], [], 0.45, RANK["N"]))
         for s in range(S, -1, -1):
             for p in range(D_PIECES):
-                deps = [("N", s)]
-                if s < S:
-                    deps += [("Z", s + 1, q) for q in range(D_PIECES)]
                 wait = [("z", s, p)] if s < S else []
                 wide = 2 if s <= WIDE_HOPS else 1
                 send = [(("z", s - 1, p), "z", wide * (zd if s < S else zd / 2))] if s else []
-                out.append((("Z", s, p), deps, wait, send, 0.15, 4))
+                out.append((("Z", s, p), [("N", s)], wait, send, 0.05, RANK["Z"]))
         return out
 
-    def schedule(self, latency=2.2, start=3.5):
+    def schedule(self, latency=2.6, start=4.0):
         ops = self.ops()
         done, arrives, free = set(), {}, {"x": 0.0, "z": 0.0}
         now, result = 0.0, []
@@ -95,17 +111,19 @@
         return result
 
 
-def kernel(plan, tok, wg, wu, wd, out, X, W, WD, GV, UV, PB, SR, RR, SD, RD, H, O, ZS, ZR, YS, YR,
+def kernel(plan, tok, wg, wu, wd, out, X, W, WD, V, PB, SR, RR, SD, RD, H, O, ZS, ZR, YS, YR,
            local_sem, send_sem, recv_sem):
     S, B = plan.S, plan.block
     ring = 2 * 2 * S
-    width = wg.shape[1]
+    width = wg.shape[0]
     grid, me = lax.axis_index("grid"), lax.axis_index("depth")
     core = lax.rem(grid, 2)
     other = 1 - core
     partner = {"grid": grid + 1 - 2 * core}
-    zway = ({"grid": lax.rem(grid + 2, ring)}, {"grid": lax.rem(grid + ring - 2, ring)})
+    chip = grid - core
+    zway = ({"grid": lax.rem(chip + 2, ring) + other}, {"grid": lax.rem(chip + ring - 2, ring) + other})
     xway = ({"depth": lax.rem(me + 1, 4)}, {"depth": lax.rem(me + 3, 4)})
+    across = {"depth": lax.rem(me + 2, 4)}
 
     numbers, started = {}, []
 
@@ -125,27 +143,27 @@
 
     loads = [
         pltpu.make_async_copy(tok, X.at[pl.ds(0, B)], local_sem.at[0]),
-        pltpu.make_async_copy(wg, GV, local_sem.at[1]),
-        pltpu.make_async_copy(wu, UV, local_sem.at[2]),
+        pltpu.make_async_copy(wg, V.at[pl.ds(0, width)], local_sem.at[1]),
+        pltpu.make_async_copy(wu, V.at[pl.ds(width, width)], local_sem.at[2]),
         pltpu.make_async_copy(wd, WD.at[core], local_sem.at[3]),
     ]
     for load in loads:
         load.start()
 
     barrier = pltpu.get_barrier_semaphore()
-    for to in (*zway, *xway, partner):
+    for to in (*zway, *xway, across, partner):
         pl.semaphore_signal(barrier, inc=1, device_id=to, device_id_type=pl.DeviceIdType.MESH)
-    pl.semaphore_wait(barrier, 5)
-
-    def a_rows(s, way, p):
-        size = B // A_PIECES
+    pl.semaphore_wait(barrier, 6)
+
+    def a_part(s, way, p):
+        size, wide = B // A_ROWS, X.shape[1] // A_COLS
         base = plan.off(s) + (B if way == 1 and 0 < s < S else 0)
-        return pl.ds(base + p * size, size)
+        return pl.ds(base + p // A_COLS * size, size), pl.ds(p % A_COLS * wide, wide)
 
     def a_send(s, p):
         for way in (0, 1):
             if p in plan.pieces(s + 1, way, A_PIECES):
-                send(("a", s + 1, way, p), X.at[a_rows(s, way, p)], X.at[a_rows(s + 1, way, p)], zway[way])
+                send(("a", s + 1, way, p), X.at[a_part(s, way, p)], X.at[a_part(s + 1, way, p)], zway[way])
 
     def op_a(s, p=None):
         if s == 0:
@@ -155,10 +173,10 @@
             for load in loads[1:3]:
                 load.wait()
 
-            @pl.loop(0, wg.shape[0] // 128)
+            @pl.loop(0, 2 * width // 128)
             def _(i):
                 r = pl.ds(pl.multiple_of(i * 128, 128), 128)
-                W[core, r, :] = jnp.concatenate([GV[r, :], UV[r, :]], axis=1)
+                W[core, :, r] = V[r, :].T
 
             send(("w",), W.at[core], W.at[core], partner)
             loads[3].wait()
@@ -166,8 +184,7 @@
             return
         for way in (0, 1):
             if p in plan.pieces(s, way, A_PIECES):
-                dst = X.at[a_rows(s, way, p)]
-                arrived(("a", s, way, p), dst, zway[way])
+                arrived(("a", s, way, p), X.at[a_part(s, way, p)], zway[way])
         if s < S:
             a_send(s, p)
 
@@ -185,9 +202,10 @@
         for half in (0, 1):
             PB[half, r, :] = jnp.dot(X[r, :], W[half], preferred_element_type=F32)
             SR[half, q, :] = PB[half, quarter(s, 2), :].astype(BF16)
-            send(("r", s, half), SR.at[half, q], RR.at[half, q], xway[half])
-        for way in (0, 1):
-            half = 1 - way
+            send(("r", s, half), SR.at[half, q], RR.at[half, q], across if plan.direct(s) else xway[half])
+        for way, half in ((0, 1), (1, 0), (0, 0), (1, 1)):
+            if way == half and not plan.direct(s):
+                continue
             SD[way, half, q, :] = PB[half, quarter(s, 1 + 2 * way), :].astype(BF16)
             send(("d", s, way, half), SD.at[way, half, q], RD.at[way, half, q], xway[way])
 
@@ -206,16 +224,21 @@
                 arrived(("d", s, way, half), RD.at[way, half, q], xway[way])
         for half in (0, 1):
             t = PB[half, mine, :] + RD[0, half, q, :].astype(F32) + RD[1, half, q, :].astype(F32)
+            if plan.direct(s):
+                arrived(("r", s, half), RR.at[half, q], across)
+                t = t + RR[half, q, :].astype(F32)
             gate, up = t[:, :width], t[:, width:]
             parts.append(gate / (1.0 + jnp.exp(-gate)) * up)
         H[mine, :] = jnp.concatenate(parts, axis=1).astype(BF16)
         for way in (0, 1):
             send(("h", s, way), H.at[mine], H.at[mine], xway[way])
+        if plan.direct(s):
+            send(("f", s), H.at[mine], H.at[mine], across)
 
     def passed_on(s, way, k):
         size = plan.rows(s) // 4
         if s in (0, S):
-            return quarter(s, k) if way == (0 if s == 0 else 1) else None
+            return quarter(s, k) if way == 0 else None
         start = plan.off(s) + lax.rem(me + k, 4) * size + way * (size // 2)
         return pl.ds(pl.multiple_of(start, 16), size // 2)
 
@@ -230,10 +253,15 @@
     def op_n(s):
         if s == plan.order()[0]:
             arrived(("v",), WD.at[other], partner)
-        for way in (0, 1):
-            part = passed_on(s, way, 2)
-            if part is not None:
-                arrived(("f", s, way), H.at[part], xway[way])
+        if plan.direct(s):
+            for way in (0, 1):
+                arrived(("h", s, way), H.at[quarter(s, 3 - 2 * way)], xway[way])
+            arrived(("f", s), H.at[quarter(s, 2)], across)
+        else:
+            for way in (0, 1):
+                part = passed_on(s, way, 2)
+                if part is not None:
+                    arrived(("f", s, way), H.at[part], xway[way])
         r = pl.ds(plan.off(s), plan.rows(s))
         depth = WD.shape[0] * WD.shape[1]
         O[r, :] = jnp.dot(H[r, :], WD[...].reshape(depth, WD.shape[2]), preferred_element_type=F32)
@@ -275,9 +303,8 @@
 
 def messages(plan):
     S = plan.S
-    a = 2 * ((S - 1) * A_PIECES + A_PIECES // 2)
-    z = 2 * ((S - 1) * D_PIECES + D_PIECES // 2)
-    return a + z + 2 + (S + 1) * 8 + 2 * (S - 1) + 2
+    rings = 2 * ((S - 1) * (A_PIECES + D_PIECES) + (A_PIECES + D_PIECES) // 2)
+    return rings + 2 + (S + 1) * 10
 
 
 def body(tokens, gate_weight, up_weight, down_weight):
@@ -297,8 +324,7 @@
             pltpu.VMEM((total, deep), BF16),
             pltpu.VMEM((2, deep, 2 * width), BF16),
             pltpu.VMEM((2, width, cols), BF16),
-            pltpu.VMEM((deep, width), BF16),
-            pltpu.VMEM((deep, width), BF16),
+            pltpu.VMEM((2 * width, deep), BF16),
             pltpu.VMEM((2, total, 2 * width), F32),
             pltpu.VMEM((2, quarters, 2 * width), BF16),
             pltpu.VMEM((2, quarters, 2 * width), BF16),
@@ -316,7 +342,7 @@
         ],
         compiler_params=pltpu.CompilerParams(
             collective_id=0, has_side_effects=True, vmem_limit_bytes=60 * 1024 * 1024),
-    )(tokens, gate_weight, up_weight, down_weight)
+    )(tokens, gate_weight.T, up_weight.T, down_weight)
 
 
 def solution(mesh):

time: 121 us -> 118 us (0.975); the launches traced: 121 us -> 116 us
  local copies, waits for them, and re-layouts: 5.22 us -> 1.57 us
    unnamed x5 -> x1, local copies, waits for them, and re-layouts: 5.22 us -> 1.57 us
    pallas_call x1, Pallas kernels: 116 us -> 115 us  [body(): pl.pallas_call(functools.partial(kernel, plan), out_shape=jax.ShapeDtypeS...]
where the time goes in v2:
time: 118 us; the launch traced here: 116 us
  Pallas kernels  115 us (97%)
  local copies, waits for them, and re-layouts  1.57 us (1%)
    pallas_call x1, Pallas kernels, body(): pl.pallas_call(functools.partial(kernel, plan), out_shape=jax.ShapeDtypeS...  115 us

profile of v2, /device:TPU:40, one launch (start us, length us, event | category | flops | bytes accessed | tf_op | source)
XLA Modules:
  0.0 116.1 jit_solution(4823824547688846871)
XLA Ops:
  0.0 114.6 %shard_map.46 = bf16[64,1024]{1,0:T(8,128)(2,1)} custom-call(bf16[64,1024]{1,0:T(8,128)(2,1)} %tok.1, bf16[448,1024]{1,0:T(8,128)(2,1)} %bitcast.2, bf16[448,1024]{1,0:T(8,128)(2,1)} %bitcast.3, bf16[448,1024]{1,0:T(8,128)(2,1)} %wd.1), custom_call_target="tpu_custom_call" | custom-call | tf_op jit(solution)/shard_map/pallas_call | solution.py:318
  114.6 1.6 %copy.6 = bf16[64,1024]{1,0:T(8,128)(2,1)} copy(bf16[64,1024]{1,0:T(8,128)(2,1)} %shard_map.46) | data formatting | bytes 262144

commit v3 on v2

--- a/solution.py
+++ b/solution.py
@@ -15,11 +15,10 @@
 A_PIECES = A_ROWS * A_COLS
 D_PIECES = 4
 WIDE_HOPS = 3
-GATES = (("M", 1), ("R", 2))
-EARLY = 5
-DIRECT = 1
-SPLIT = False
-RANK = {"A": 0, "M": 6, "D": 5, "R": 1, "S": 2, "F": 1, "N": 5, "Z": 4}
+
+SEQUENCE = (0, 1, 5, 6, 7, 8, 4, 3, 2)
+GATES = (("M", 2), ("R", 2), ("M", 2), ("R", 3), ("R", 3), ("M", 3), ("F", 3), ("F", 3), ("R", 2))
+RANK = {"A": 0, "M": 4, "R": 3, "S": 5, "F": 5, "N": 1, "Z": 0}
 
 
 class Plan:
@@ -35,11 +34,12 @@
         return self.block if s in (0, self.S) else 2 * self.block
 
     def direct(self, s):
-        return s > self.S - DIRECT
+        return s == self.S
 
     def order(self):
-        early = min(EARLY, self.S)
-        return list(range(early)) + list(range(self.S, early - 1, -1))
+        if len(SEQUENCE) == self.S + 1:
+            return list(zip(SEQUENCE, GATES))
+        return [(s, None) for s in [0, *range(self.S, 0, -1)]]
 
     def pieces(self, s, way, n):
         if s < self.S:
@@ -49,62 +49,66 @@
     def ops(self):
         S, out = self.S, []
         za, zd = 2.8 / A_PIECES, 2.8 / D_PIECES
-        out.append((("A", 0, 0), [], [], [(("a", 1, p), "z", za) for p in range(A_PIECES)], 1.0, RANK["A"]))
+        out.append((("A", 0, 0), [], [], [(("a", 1, p), "z", za) for p in range(A_PIECES)], 1.0))
         for s in range(1, S + 1):
             for p in range(A_PIECES):
                 send = [(("a", s + 1, p), "z", za if s + 1 < S else za / 2)] if s < S else []
-                out.append((("A", s, p), [("A", 0, 0)], [("a", s, p)], send, 0.04, RANK["A"]))
-        seq = self.order()
-        for i, s in enumerate(seq):
-            u = self.rows(s) / (2 * self.block)
+                out.append((("A", s, p), [("A", 0, 0)], [("a", s, p)], send, 0.04))
+        order = self.order()
+        for i, (s, gate) in enumerate(order):
+            x = 1.23 * self.rows(s) / (2 * self.block)
             deps = [("A", s, p) for p in range(A_PIECES)] if s else [("A", 0, 0)]
             if i:
-                deps.append(("M", seq[i - 1]))
-            stage, lag = GATES[i > EARLY]
-            if i >= lag and not (stage == "R" and self.direct(seq[i - lag])):
-                deps.append((stage, seq[i - lag]))
-            x = 1.23 * u
-            if self.direct(s):
-                out.append((("M", s), deps, [], [(("r", s), "x", 2 * x), (("d", s), "x", 2 * x)], 1.0, RANK["M"]))
-                out.append((("S", s), [("M", s)], [("r", s), ("d", s)], [(("h", s), "x", 2 * x)], 0.2, RANK["S"]))
-                out.append((("N", s), [("S", s)], [("h", s)], [], 0.45, RANK["N"]))
+                deps.append(("M", order[i - 1][0], 1))
+            if gate and i >= gate[1]:
+                stage, t = gate[0], order[i - gate[1]][0]
+                if not (stage in "RF" and self.direct(t)):
+                    deps += [(stage, t, 0), (stage, t, 1)] if stage in "RFM" else [(stage, t)]
+            across = self.direct(s)
+            for h in (0, 1):
+                send = [(("r", s, h), ("x", h), 2 * x if across else x), (("d", s, 1 - h, h), ("x", 1 - h), x)]
+                if across:
+                    send.append((("d", s, h, h), ("x", h), x))
+                out.append((("M", s, h), [("M", s, 0)] if h else deps, [], send, 0.52))
+            parts = [("d", s, w, h) for w in (0, 1) for h in (0, 1)]
+            if across:
+                send = [(("h", s, w), ("x", w), 2 * x) for w in (0, 1)]
+                out.append((("S", s), [("M", s, 1)], parts + [("r", s, 0), ("r", s, 1)], send, 0.2))
+                out.append((("N", s), [("S", s)], [("h", s, 0), ("h", s, 1)], [], 0.45))
                 continue
-            if SPLIT:
-                out.append((("M", s), deps, [], [(("r", s), "x", x)], 1.0, RANK["M"]))
-                out.append((("D", s), [("M", s)], [], [(("d", s), "x", x)], 0.03, RANK["D"]))
-            else:
-                out.append((("M", s), deps, [], [(("r", s), "x", x), (("d", s), "x", x)], 1.0, RANK["M"]))
-            out.append((("R", s), [("M", s)], [("r", s)], [(("e", s), "x", x)], 0.05, RANK["R"]))
-            out.append((("S", s), [("R", s)] + [("D", s)] * SPLIT, [("d", s), ("e", s)], [(("h", s), "x", x)], 0.2, RANK["S"]))
-            out.append((("F", s), [("S", s)], [("h", s)], [(("f", s), "x", x / 2)], 0.02, RANK["F"]))
-            out.append((("N", s), [("F", s)], [("f", s)], [], 0.45, RANK["N"]))
+            for w in (0, 1):
+                out.append((("R", s, w), [("M", s, 1)], [("r", s, w)], [(("d", s, w, w), ("x", w), x)], 0.03))
+            send = [(("h", s, w), ("x", w), x) for w in (0, 1)]
+            out.append((("S", s), [("R", s, 0), ("R", s, 1)], parts, send, 0.2))
+            for w in (0, 1):
+                out.append((("F", s, w), [("S", s)], [("h", s, w)], [(("f", s, w), ("x", w), x / 2)], 0.02))
+            out.append((("N", s), [("F", s, 0), ("F", s, 1)], [("f", s, 0), ("f", s, 1)], [], 0.45))
         for s in range(S, -1, -1):
             for p in range(D_PIECES):
-                wait = [("z", s, p)] if s < S else []
                 wide = 2 if s <= WIDE_HOPS else 1
                 send = [(("z", s - 1, p), "z", wide * (zd if s < S else zd / 2))] if s else []
-                out.append((("Z", s, p), [("N", s)], wait, send, 0.05, RANK["Z"]))
+                out.append((("Z", s, p), [("N", s)], [("z", s, p)] if s < S else [], send, 0.05))
         return out
 
     def schedule(self, latency=2.6, start=4.0):
         ops = self.ops()
-        done, arrives, free = set(), {}, {"x": 0.0, "z": 0.0}
+        done, arrives, free = set(), {}, {}
         now, result = 0.0, []
         while ops:
             best = None
-            for k, (name, deps, wait, send, cost, rank) in enumerate(ops):
+            for k, (name, deps, wait, send, cost) in enumerate(ops):
                 if any(d not in done for d in deps) or any(m not in arrives for m in wait):
                     continue
                 ready = max([now] + [arrives[m] for m in wait])
                 if name[0] == "M":
                     ready = max(ready, start)
-                key = (ready, rank, k)
+                key = (ready, RANK[name[0]], k)
                 if best is None or key < best[0]:
                     best = (key, k)
-            name, deps, wait, send, cost, rank = ops.pop(best[1])
+            name, deps, wait, send, cost = ops.pop(best[1])
             now = best[0][0] + cost
             for message, link, length in send:
-                free[link] = max(free[link], now) + length
+                free[link] = max(free.get(link, 0.0), now) + length
                 arrives[message] = free[link] + latency
             done.add(name)
             result.append((name, round(now, 2)))
@@ -195,26 +199,25 @@
     def packed(s):
         return pl.ds(plan.off(s) // 4, plan.rows(s) // 4)
 
-    def op_m(s):
-        if s == 0:
+    pending = {"w", "v"}
+
+    def op_m(s, half):
+        if "w" in pending:
+            pending.remove("w")
             arrived(("w",), W.at[other], partner)
         r, q = pl.ds(plan.off(s), plan.rows(s)), packed(s)
-        for half in (0, 1):
-            PB[half, r, :] = jnp.dot(X[r, :], W[half], preferred_element_type=F32)
-            SR[half, q, :] = PB[half, quarter(s, 2), :].astype(BF16)
-            send(("r", s, half), SR.at[half, q], RR.at[half, q], across if plan.direct(s) else xway[half])
-        for way, half in ((0, 1), (1, 0), (0, 0), (1, 1)):
-            if way == half and not plan.direct(s):
-                continue
+        PB[half, r, :] = jnp.dot(X[r, :], W[half], preferred_element_type=F32)
+        SR[half, q, :] = PB[half, quarter(s, 2), :].astype(BF16)
+        send(("r", s, half), SR.at[half, q], RR.at[half, q], across if plan.direct(s) else xway[half])
+        for way in (1 - half, half) if plan.direct(s) else (1 - half,):
             SD[way, half, q, :] = PB[half, quarter(s, 1 + 2 * way), :].astype(BF16)
             send(("d", s, way, half), SD.at[way, half, q], RD.at[way, half, q], xway[way])
 
-    def op_r(s):
+    def op_r(s, way):
         q = packed(s)
-        for way in (0, 1):
-            arrived(("r", s, way), RR.at[way, q], xway[way])
-            SD[way, way, q, :] = (PB[way, quarter(s, 1 + 2 * way), :] + RR[way, q, :].astype(F32)).astype(BF16)
-            send(("d", s, way, way), SD.at[way, way, q], RD.at[way, way, q], xway[way])
+        arrived(("r", s, way), RR.at[way, q], xway[way])
+        SD[way, way, q, :] = (PB[way, quarter(s, 1 + 2 * way), :] + RR[way, q, :].astype(F32)).astype(BF16)
+        send(("d", s, way, way), SD.at[way, way, q], RD.at[way, way, q], xway[way])
 
     def op_s(s):
         q, mine = packed(s), quarter(s, 0)
@@ -237,21 +240,21 @@
 
     def passed_on(s, way, k):
         size = plan.rows(s) // 4
-        if s in (0, S):
+        if s == 0:
             return quarter(s, k) if way == 0 else None
         start = plan.off(s) + lax.rem(me + k, 4) * size + way * (size // 2)
         return pl.ds(pl.multiple_of(start, 16), size // 2)
 
-    def op_f(s):
-        for way in (0, 1):
-            k = 3 - 2 * way
-            arrived(("h", s, way), H.at[quarter(s, k)], xway[way])
-            part = passed_on(s, way, k)
-            if part is not None:
-                send(("f", s, way), H.at[part], H.at[part], xway[way])
+    def op_f(s, way):
+        k = 3 - 2 * way
+        arrived(("h", s, way), H.at[quarter(s, k)], xway[way])
+        part = passed_on(s, way, k)
+        if part is not None:
+            send(("f", s, way), H.at[part], H.at[part], xway[way])
 
     def op_n(s):
-        if s == plan.order()[0]:
+        if "v" in pending:
+            pending.remove("v")
             arrived(("v",), WD.at[other], partner)
         if plan.direct(s):
             for way in (0, 1):
@@ -317,7 +320,7 @@
     n = messages(plan)
     return pl.pallas_call(
         functools.partial(kernel, plan),
-        out_shape=jax.ShapeDtypeStruct((block, cols), BF16),
+        out_shape=pltpu.VMEM((block, cols), BF16),
         in_specs=[any_] * 4,
         out_specs=vmem,
         scratch_shapes=[

time: 118 us -> 112 us (0.949)
  Pallas kernels: 115 us -> 111 us
    pallas_call x1, Pallas kernels: 115 us -> 111 us  [body(): pl.pallas_call(functools.partial(kernel, plan), out_shape=pltpu.VMEM((blo...]
where the time goes in v3:
time: 112 us; the launch traced here: 111 us
  Pallas kernels  111 us (99%)
    pallas_call x1, Pallas kernels, body(): pl.pallas_call(functools.partial(kernel, plan), out_shape=pltpu.VMEM((blo...  111 us

profile of v3, /device:TPU:40, one launch (start us, length us, event | category | flops | bytes accessed | tf_op | source)
XLA Modules:
  0.0 111.3 jit_solution(5898831836059525217)
XLA Ops:
  0.0 110.6 %shard_map.46 = bf16[64,1024]{1,0:T(8,128)(2,1)S(1)} custom-call(bf16[64,1024]{1,0:T(8,128)(2,1)} %tok.1, bf16[448,1024]{1,0:T(8,128)(2,1)} %bitcast.2, bf16[448,1024]{1,0:T(8,128)(2,1)} %bitcast.3, bf16[448,1024]{1,0:T(8,128)(2,1)} %wd.1), custom_call_target="tpu_custom_call" | custom-call | tf_op jit(solution)/shard_map/pallas_call | solution.py:321
  110.6 0.7 copy.6

commit v4 on v3

v4 whole, which is shorter than its diff:
```python
import functools
import heapq

import jax
import jax.numpy as jnp
from jax import lax
from jax.experimental import pallas as pl
from jax.experimental.pallas import tpu as pltpu
from jax.sharding import PartitionSpec as P

F32 = jnp.float32
BF16 = jnp.bfloat16

A_ROWS = 4
A_COLS = 2
A_PIECES = A_ROWS * A_COLS
D_PIECES = 4
WIDE_HOPS = 3
CUT = 512

SEQUENCE = (
    (0, 0), (1, 1), (3, 1), (4, 1), (5, 0), (5, 1), (6, 0), (7, 1), (7, 0), (6, 1), (8, 0), (4, 0), (3, 0), (2, 0),
    (2, 1), (1, 0),
)
GATES = (
    ("R", 3), None, ("R", 1), ("S", 3), ("F", 1), ("F", 3), None, ("M", 3), ("M", 4), ("R", 3), ("R", 2), ("F", 3),
    ("N", 4), ("R", 2), ("S", 2), ("M", 3),
)
DIRECT = (
    (0, 0), (1, 0), (1, 1), (2, 0), (2, 1), (3, 0), (3, 1), (4, 0), (4, 1), (8, 0),
)
RANK = {"A": 0, "M": 2, "R": 5, "S": 2, "F": 5, "N": 6, "Z": 0}


class Plan:
    def __init__(self, chips, block):
        self.S = chips // 2
        self.block = block
        self.total = block * chips
        self.blocks = [(0, 0), *((s, w) for s in range(1, self.S) for w in (0, 1)), (self.S, 0)]

    def off(self, b):
        return self.block * self.blocks.index(b)

    def order(self):
        if len(SEQUENCE) == len(self.blocks):
            return list(zip(SEQUENCE, GATES))
        return [(b, None) for b in self.blocks[:1] + self.blocks[:0:-1]]

    def pieces(self, s, way, n):
        if s < self.S:
            return range(n)
        return range(n // 2) if way == 0 else range(n // 2, n)

    def ops(self):
        S, out = self.S, []
        za, zd, x = 2.8 / A_PIECES, 2.8 / D_PIECES, 0.615
        first = ("A", 0, 0, 0)
        out.append((first, [], [], [(("a", 1, w, p), ("z", w), za) for p in range(A_PIECES) for w in (0, 1)], 0.9))
        for s in range(1, S + 1):
            for p in range(A_PIECES):
                for w in (0, 1):
                    if p in self.pieces(s, w, A_PIECES):
                        on = s < S and p in self.pieces(s + 1, w, A_PIECES)
                        send = [(("a", s + 1, w, p), ("z", w), za)] if on else []
                        out.append((("A", s, w, p), [first], [("a", s, w, p)], send, 0.03))
        order = self.order()
        for i, (b, gate) in enumerate(order):
            s, w = b
            if s == 0:
                deps = [first]
            else:
                ways = (w,) if s < S else (0, 1)
                deps = [("A", s, v, p) for v in ways for p in self.pieces(s, v, A_PIECES)]
            if i:
                deps.append(("M", order[i - 1][0], 1, 1))
            if gate and i >= gate[1]:
                stage, t = gate[0], order[i - gate[1]][0]
                if stage == "M":
                    deps.append(("M", t, 1, 1))
                elif stage in "SN":
                    deps.append((stage, t))
                elif t not in DIRECT:
                    deps += [("R", t, 0), ("R", t, 1)] if stage == "R" else [("F", t)]
            across = b in DIRECT
            for h in (0, 1):
                send = [(("r", b, h), ("x", h), 2 * x if across else x), (("d", b, 1 - h, h), ("x", 1 - h), x)]
                if across:
                    send.append((("d", b, h, h), ("x", h), x))
                out.append((("M", b, h, 0), [("M", b, 0, 1)] if h else deps, [], [], 0.29))
                out.append((("M", b, h, 1), [("M", b, h, 0)], [], send, 0.24))
            parts = [("d", b, v, h) for v in (0, 1) for h in (0, 1)]
            if across:
                send = [(("h", b, v), ("x", v), 2 * x) for v in (0, 1)]
                out.append((("S", b), [("M", b, 1, 1)], parts + [("r", b, 0), ("r", b, 1)], send, 0.12))
                out.append((("N", b), [("S", b)], [("h", b, 0), ("h", b, 1)], [], 0.45))
                continue
            for v in (0, 1):
                out.append((("R", b, v), [("M", b, 1, 1)], [("r", b, v)], [(("d", b, v, v), ("x", v), x)], 0.03))
            send = [(("h", b, v), ("x", v), x) for v in (0, 1)]
            out.append((("S", b), [("R", b, 0), ("R", b, 1)], parts, send, 0.12))
            out.append((("F", b), [("S", b)], [("h", b, w)], [(("f", b), ("x", w), x)], 0.02))
            out.append((("N", b), [("F", b)], [("f", b), ("h", b, 1 - w)], [], 0.45))
        for s in range(S, 0, -1):
            for p in range(D_PIECES):
                for w in (0, 1):
                    if p in self.pieces(s, w, D_PIECES):
                        wait = [("z", s, w, p)] if s < S and p in self.pieces(s + 1, w, D_PIECES) else []
                        send = [(("z", s - 1, w, p), ("z", w), 2 * zd if s <= WIDE_HOPS else zd)]
                        out.append((("Z", s, w, p), [("N", (s, 1 - w if s < S else 0))], wait, send, 0.04))
        for p in range(D_PIECES):
            out.append((("Z", 0, 0, p), [("N", (0, 0))], [("z", 0, 0, p), ("z", 0, 1, p)], [], 0.05))
        return out

    def schedule(self, latency=2.6, start=4.0):
        ops = self.ops()
        left = [len(op[1]) + len(op[2]) for op in ops]
        ready, free, users = [0.0] * len(ops), {}, {}
        for i, op in enumerate(ops):
            for key in op[1] + op[2]:
                users.setdefault(key, []).append(i)
        later, now_ready, now, names = [], [], 0.0, []

        def enter(i):
            at = max(ready[i], start) if ops[i][0][0] == "M" else ready[i]
            heapq.heappush(later, (at, RANK[ops[i][0][0]], i))

        for i in range(len(ops)):
            if not left[i]:
                enter(i)
        while later or now_ready:
            while later and later[0][0] <= now:
                _, rank, i = heapq.heappop(later)
                heapq.heappush(now_ready, (rank, i))
            if not now_ready:
                now = later[0][0]
                continue
            name, _, _, sends, cost = ops[heapq.heappop(now_ready)[1]]
            now += cost
            names.append((name, now))
            known = [(name, 0.0)]
            for key, link, length in sends:
                free[link] = max(free.get(link, 0.0), now) + length
                known.append((key, free[link] + latency))
            for key, at in known:
                for i in users.get(key, ()):
                    left[i] -= 1
                    ready[i] = max(ready[i], at)
                    if not left[i]:
                        enter(i)
        return names


def kernel(plan, tok, wg, wu, wd, out, X, W, WD, V, PB, SR, RR, SD, RD, H, O, ZS, ZR, YS, YR,
           local_sem, send_sem, recv_sem):
    S, B = plan.S, plan.block
    ring = 2 * 2 * S
    width = wg.shape[0]
    grid, me = lax.axis_index("grid"), lax.axis_index("depth")
    core = lax.rem(grid, 2)
    other = 1 - core
    partner = {"grid": grid + 1 - 2 * core}
    chip = grid - core
    zway = ({"grid": lax.rem(chip + 2, ring) + other}, {"grid": lax.rem(chip + ring - 2, ring) + other})
    xway = ({"depth": lax.rem(me + 1, 4)}, {"depth": lax.rem(me + 3, 4)})
    across = {"depth": lax.rem(me + 2, 4)}

    numbers, started = {}, []

    def message(key, src, dst, to):
        n = numbers.setdefault(key, len(numbers))
        return pltpu.make_async_remote_copy(
            src_ref=src, dst_ref=dst, send_sem=send_sem.at[n], recv_sem=recv_sem.at[n],
            device_id=to, device_id_type=pl.DeviceIdType.MESH)

    def send(key, src, dst, to):
        m = message(key, src, dst, to)
        m.start()
        started.append(m)

    def arrived(key, dst, to):
        message(key, dst, dst, to).wait_recv()

    loads = [
        pltpu.make_async_copy(tok, X.at[pl.ds(0, B)], local_sem.at[0]),
        pltpu.make_async_copy(wg, V.at[pl.ds(0, width)], local_sem.at[1]),
        pltpu.make_async_copy(wu, V.at[pl.ds(width, width)], local_sem.at[2]),
        pltpu.make_async_copy(wd, WD.at[core], local_sem.at[3]),
    ]
    for load in loads:
        load.start()

    barrier = pltpu.get_barrier_semaphore()
    for to in (*zway, *xway, across, partner):
        pl.semaphore_signal(barrier, inc=1, device_id=to, device_id_type=pl.DeviceIdType.MESH)
    pl.semaphore_wait(barrier, 6)

    def a_part(s, way, p):
        size, wide = B // A_ROWS, X.shape[1] // A_COLS
        base = plan.off((s, way if 0 < s < S else 0))
        return pl.ds(base + p // A_COLS * size, size), pl.ds(p % A_COLS * wide, wide)

    def a_send(s, way, p):
        if s < S and p in plan.pieces(s + 1, way, A_PIECES):
            send(("a", s + 1, way, p), X.at[a_part(s, way, p)], X.at[a_part(s + 1, way, p)], zway[way])

    def op_a(s, way, p):
        if s == 0:
            loads[0].wait()
            for p in range(A_PIECES):
                for way in (0, 1):
                    a_send(0, way, p)
            for load in loads[1:3]:
                load.wait()

            @pl.loop(0, 2 * width // 128)
            def _(i):
                r = pl.ds(pl.multiple_of(i * 128, 128), 128)
                W[core, :, r] = V[r, :].T

            send(("w",), W.at[core], W.at[core], partner)
            loads[3].wait()
            send(("v",), WD.at[core], WD.at[core], partner)
            return
        arrived(("a", s, way, p), X.at[a_part(s, way, p)], zway[way])
        a_send(s, way, p)

    size = B // 4

    def quarter(b, k):
        return pl.ds(pl.multiple_of(plan.off(b) + lax.rem(me + k, 4) * size, 16), size)

    def packed(b):
        return pl.ds(plan.off(b) // 4, size)

    pending = {"w", "v"}

    def op_m(b, half, part):
        if "w" in pending:
            pending.remove("w")
            arrived(("w",), W.at[other], partner)
        r, q = pl.ds(plan.off(b), B), packed(b)
        cut = min(CUT, width)
        cols = pl.ds(0, cut) if part == 0 else pl.ds(cut, 2 * width - cut)
        PB[half, r, cols] = jnp.dot(X[r, :], W[half, :, cols], preferred_element_type=F32)
        if part == 0:
            return
        SR[half, q, :] = PB[half, quarter(b, 2), :].astype(BF16)
        send(("r", b, half), SR.at[half, q], RR.at[half, q], across if b in DIRECT else xway[half])
        for way in (1 - half, half) if b in DIRECT else (1 - half,):
            SD[way, half, q, :] = PB[half, quarter(b, 1 + 2 * way), :].astype(BF16)
            send(("d", b, way, half), SD.at[way, half, q], RD.at[way, half, q], xway[way])

    def op_r(b, way):
        q = packed(b)
        arrived(("r", b, way), RR.at[way, q], xway[way])
        SD[way, way, q, :] = (PB[way, quarter(b, 1 + 2 * way), :] + RR[way, q, :].astype(F32)).astype(BF16)
        send(("d", b, way, way), SD.at[way, way, q], RD.at[way, way, q], xway[way])

    def op_s(b):
        q, mine = packed(b), quarter(b, 0)
        parts = []
        for way in (0, 1):
            for half in (0, 1):
                arrived(("d", b, way, half), RD.at[way, half, q], xway[way])
        for half in (0, 1):
            t = PB[half, mine, :] + RD[0, half, q, :].astype(F32) + RD[1, half, q, :].astype(F32)
            if b in DIRECT:
                arrived(("r", b, half), RR.at[half, q], across)
                t = t + RR[half, q, :].astype(F32)
            gate, up = t[:, :width], t[:, width:]
            parts.append(gate / (1.0 + jnp.exp(-gate)) * up)
        H[mine, :] = jnp.concatenate(parts, axis=1).astype(BF16)
        for way in (0, 1):
            send(("h", b, way), H.at[mine], H.at[mine], xway[way])
        if b in DIRECT:
            send(("f", b), H.at[mine], H.at[mine], across)

    def op_f(b):
        way = b[1]
        rows = H.at[quarter(b, 3 - 2 * way)]
        arrived(("h", b, way), rows, xway[way])
        send(("f", b), rows, rows, xway[way])

    def op_n(b):
        if "v" in pending:
            pending.remove("v")
            arrived(("v",), WD.at[other], partner)
        for way in (0, 1):
            if b in DIRECT or way != b[1]:
                arrived(("h", b, way), H.at[quarter(b, 3 - 2 * way)], xway[way])
        arrived(("f", b), H.at[quarter(b, 2)], across if b in DIRECT else xway[b[1]])
        r = pl.ds(plan.off(b), B)
        depth = WD.shape[0] * WD.shape[1]
        O[r, :] = jnp.dot(H[r, :], WD[...].reshape(depth, WD.shape[2]), preferred_element_type=F32)

    def z_place(s, way, p):
        size = B // D_PIECES
        r = pl.ds(s * B + p * size, size)
        return (YS.at[way, r], YR.at[way, r]) if s < WIDE_HOPS else (ZS.at[way, r], ZR.at[way, r])

    def op_z(s, way, p):
        rows = B // D_PIECES
        total = O[pl.ds(plan.off((s, 1 - way if 0 < s < S else 0)) + p * rows, rows), :]
        for v in (0, 1) if s == 0 else (way,):
            if s < S and p in plan.pieces(s + 1, v, D_PIECES):
                got = z_place(s, v, p)[1]
                arrived(("z", s, v, p), got, zway[v])
                total = total + got[...].astype(F32)
        if s == 0:
            out[pl.ds(p * rows, rows), :] = total.astype(BF16)
            return
        src, dst = z_place(s - 1, way, p)
        src[...] = total.astype(src.dtype)
        send(("z", s - 1, way, p), src, dst, zway[way])

    run = {"A": op_a, "M": op_m, "R": op_r, "S": op_s, "F": op_f, "N": op_n, "Z": op_z}
    for (name, *at), _ in plan.schedule():
        run[name](*at)
    for m in started:
        m.wait_send()


def messages(plan):
    S = plan.S
    rings = 2 * ((S - 1) * (A_PIECES + D_PIECES) + (A_PIECES + D_PIECES) // 2)
    return rings + 2 + 2 * S * 9


def body(tokens, gate_weight, up_weight, down_weight):
    block, deep = tokens.shape
    width, cols = down_weight.shape
    chips = lax.axis_size("grid") // 2
    plan = Plan(chips, block)
    total, quarters = plan.total, plan.total // 4
    vmem, any_ = pl.BlockSpec(memory_space=pltpu.VMEM), pl.BlockSpec(memory_space=pl.ANY)
    n = messages(plan)
    return pl.pallas_call(
        functools.partial(kernel, plan),
        out_shape=pltpu.VMEM((block, cols), BF16),
        in_specs=[any_] * 4,
        out_specs=vmem,
        scratch_shapes=[
            pltpu.VMEM((total, deep), BF16),
            pltpu.VMEM((2, deep, 2 * width), BF16),
            pltpu.VMEM((2, width, cols), BF16),
            pltpu.VMEM((2 * width, deep), BF16),
            pltpu.VMEM((2, total, 2 * width), F32),
            pltpu.VMEM((2, quarters, 2 * width), BF16),
            pltpu.VMEM((2, quarters, 2 * width), BF16),
            pltpu.VMEM((2, 2, quarters, 2 * width), BF16),
            pltpu.VMEM((2, 2, quarters, 2 * width), BF16),
            pltpu.VMEM((total, 2 * width), BF16),
            pltpu.VMEM((total, cols), F32),
            pltpu.VMEM((2, total // 2, cols), BF16),
            pltpu.VMEM((2, total // 2, cols), BF16),
            pltpu.VMEM((2, max(1, WIDE_HOPS) * block, cols), F32),
            pltpu.VMEM((2, max(1, WIDE_HOPS) * block, cols), F32),
            pltpu.SemaphoreType.DMA((4,)),
            pltpu.SemaphoreType.DMA((n,)),
            pltpu.SemaphoreType.DMA((n,)),
        ],
        compiler_params=pltpu.CompilerParams(
            collective_id=0, has_side_effects=True, vmem_limit_bytes=60 * 1024 * 1024),
    )(tokens, gate_weight.T, up_weight.T, down_weight)


def solution(mesh):
    return jax.shard_map(
        body,
        mesh=mesh,
        in_specs=(P(("groups", "grid"), "depth"), P("depth", "grid"), P("depth", "grid"), P("grid", "depth")),
        out_specs=P(("groups", "grid"), "depth"),
        check_vma=False,
    )
```

time: 112 us -> 115 us (1.027)
  Pallas kernels: 111 us -> 114 us
    pallas_call x1, Pallas kernels: 111 us -> 114 us  [body(): pl.pallas_call(functools.partial(kernel, plan), out_shape=pltpu.VMEM((blo...]
where the time goes in v4:
time: 115 us; the launch traced here: 114 us
  Pallas kernels  114 us (99%)
    pallas_call x1, Pallas kernels, body(): pl.pallas_call(functools.partial(kernel, plan), out_shape=pltpu.VMEM((blo...  114 us

profile of v4, /device:TPU:40, one launch (start us, length us, event | category | flops | bytes accessed | tf_op | source)
XLA Modules:
  0.0 114.3 jit_solution(14643797119687239666)
XLA Ops:
  0.0 113.7 %shard_map.46 = bf16[64,1024]{1,0:T(8,128)(2,1)S(1)} custom-call(bf16[64,1024]{1,0:T(8,128)(2,1)} %tok.1, bf16[448,1024]{1,0:T(8,128)(2,1)} %bitcast.2, bf16[448,1024]{1,0:T(8,128)(2,1)} %bitcast.3, bf16[448,1024]{1,0:T(8,128)(2,1)} %wd.1), custom_call_target="tpu_custom_call" | custom-call | tf_op jit(solution)/shard_map/pallas_call | solution.py:338
  113.7 0.7 copy.6

commit v5 on v4

--- a/solution.py
+++ b/solution.py
@@ -15,21 +15,20 @@
 A_COLS = 2
 A_PIECES = A_ROWS * A_COLS
 D_PIECES = 4
-WIDE_HOPS = 3
-CUT = 512
+WIDE_HOPS = 2
 
 SEQUENCE = (
-    (0, 0), (1, 1), (3, 1), (4, 1), (5, 0), (5, 1), (6, 0), (7, 1), (7, 0), (6, 1), (8, 0), (4, 0), (3, 0), (2, 0),
-    (2, 1), (1, 0),
+    (0, 0), (1, 1), (3, 1), (4, 1), (5, 1), (5, 0), (6, 0), (7, 1), (7, 0), (6, 1), (8, 0), (4, 0), (3, 0), (2, 1),
+    (2, 0), (1, 0),
 )
 GATES = (
-    ("R", 3), None, ("R", 1), ("S", 3), ("F", 1), ("F", 3), None, ("M", 3), ("M", 4), ("R", 3), ("R", 2), ("F", 3),
-    ("N", 4), ("R", 2), ("S", 2), ("M", 3),
+    ("R", 1), ("F", 2), ("S", 3), ("M", 2), ("N", 3), ("M", 3), None, ("M", 4), None, ("R", 2), ("R", 4), ("F", 3),
+    ("N", 4), ("N", 4), ("N", 4), ("S", 1),
 )
 DIRECT = (
     (0, 0), (1, 0), (1, 1), (2, 0), (2, 1), (3, 0), (3, 1), (4, 0), (4, 1), (8, 0),
 )
-RANK = {"A": 0, "M": 2, "R": 5, "S": 2, "F": 5, "N": 6, "Z": 0}
+RANK = {"A": 0, "M": 4, "R": 2, "S": 6, "F": 3, "N": 5, "Z": 3}
 
 
 class Plan:
@@ -73,11 +72,11 @@
                 ways = (w,) if s < S else (0, 1)
                 deps = [("A", s, v, p) for v in ways for p in self.pieces(s, v, A_PIECES)]
             if i:
-                deps.append(("M", order[i - 1][0], 1, 1))
+                deps.append(("M", order[i - 1][0], 1))
             if gate and i >= gate[1]:
                 stage, t = gate[0], order[i - gate[1]][0]
                 if stage == "M":
-                    deps.append(("M", t, 1, 1))
+                    deps.append(("M", t, 1))
                 elif stage in "SN":
                     deps.append((stage, t))
                 elif t not in DIRECT:
@@ -87,18 +86,17 @@
                 send = [(("r", b, h), ("x", h), 2 * x if across else x), (("d", b, 1 - h, h), ("x", 1 - h), x)]
                 if across:
                     send.append((("d", b, h, h), ("x", h), x))
-                out.append((("M", b, h, 0), [("M", b, 0, 1)] if h else deps, [], [], 0.29))
-                out.append((("M", b, h, 1), [("M", b, h, 0)], [], send, 0.24))
+                out.append((("M", b, h), [("M", b, 0)] if h else deps, [], send, 0.5))
             parts = [("d", b, v, h) for v in (0, 1) for h in (0, 1)]
             if across:
                 send = [(("h", b, v), ("x", v), 2 * x) for v in (0, 1)]
-                out.append((("S", b), [("M", b, 1, 1)], parts + [("r", b, 0), ("r", b, 1)], send, 0.12))
+                out.append((("S", b), [("M", b, 1)], parts + [("r", b, 0), ("r", b, 1)], send, 0.25))
                 out.append((("N", b), [("S", b)], [("h", b, 0), ("h", b, 1)], [], 0.45))
                 continue
             for v in (0, 1):
-                out.append((("R", b, v), [("M", b, 1, 1)], [("r", b, v)], [(("d", b, v, v), ("x", v), x)], 0.03))
+                out.append((("R", b, v), [("M", b, 1)], [("r", b, v)], [(("d", b, v, v), ("x", v), x)], 0.03))
             send = [(("h", b, v), ("x", v), x) for v in (0, 1)]
-            out.append((("S", b), [("R", b, 0), ("R", b, 1)], parts, send, 0.12))
+            out.append((("S", b), [("R", b, 0), ("R", b, 1)], parts, send, 0.17))
             out.append((("F", b), [("S", b)], [("h", b, w)], [(("f", b), ("x", w), x)], 0.02))
             out.append((("N", b), [("F", b)], [("f", b), ("h", b, 1 - w)], [], 0.45))
         for s in range(S, 0, -1):
@@ -235,16 +233,12 @@
 
     pending = {"w", "v"}
 
-    def op_m(b, half, part):
+    def op_m(b, half):
         if "w" in pending:
             pending.remove("w")
             arrived(("w",), W.at[other], partner)
         r, q = pl.ds(plan.off(b), B), packed(b)
-        cut = min(CUT, width)
-        cols = pl.ds(0, cut) if part == 0 else pl.ds(cut, 2 * width - cut)
-        PB[half, r, cols] = jnp.dot(X[r, :], W[half, :, cols], preferred_element_type=F32)
-        if part == 0:
-            return
+        PB[half, r, :] = jnp.dot(X[r, :], W[half], preferred_element_type=F32)
         SR[half, q, :] = PB[half, quarter(b, 2), :].astype(BF16)
         send(("r", b, half), SR.at[half, q], RR.at[half, q], across if b in DIRECT else xway[half])
         for way in (1 - half, half) if b in DIRECT else (1 - half,):

time: 115 us -> 109 us (0.948)
  Pallas kernels: 114 us -> 108 us
    pallas_call x1, Pallas kernels: 114 us -> 108 us  [body(): pl.pallas_call(functools.partial(kernel, plan), out_shape=pltpu.VMEM((blo...]
where the time goes in v5:
time: 109 us; the launch traced here: 108 us
  Pallas kernels  108 us (99%)
    pallas_call x1, Pallas kernels, body(): pl.pallas_call(functools.partial(kernel, plan), out_shape=pltpu.VMEM((blo...  108 us

profile of v5, /device:TPU:40, one launch (start us, length us, event | category | flops | bytes accessed | tf_op | source)
XLA Modules:
  0.0 108.4 jit_solution(17280538642751628467)
XLA Ops:
  0.0 107.7 %shard_map.46 = bf16[64,1024]{1,0:T(8,128)(2,1)S(1)} custom-call(bf16[64,1024]{1,0:T(8,128)(2,1)} %tok.1, bf16[448,1024]{1,0:T(8,128)(2,1)} %bitcast.2, bf16[448,1024]{1,0:T(8,128)(2,1)} %bitcast.3, bf16[448,1024]{1,0:T(8,128)(2,1)} %wd.1), custom_call_target="tpu_custom_call" | custom-call | tf_op jit(solution)/shard_map/pallas_call | solution.py:332
  107.7 0.7 copy.6

commit v6 on v5

--- a/solution.py
+++ b/solution.py
@@ -14,21 +14,23 @@
 A_ROWS = 4
 A_COLS = 2
 A_PIECES = A_ROWS * A_COLS
-D_PIECES = 4
+D_ROWS = 4
+D_COLS = 2
+D_PIECES = D_ROWS * D_COLS
 WIDE_HOPS = 2
 
 SEQUENCE = (
-    (0, 0), (1, 1), (3, 1), (4, 1), (5, 1), (5, 0), (6, 0), (7, 1), (7, 0), (6, 1), (8, 0), (4, 0), (3, 0), (2, 1),
+    (0, 0), (1, 1), (3, 1), (4, 1), (5, 1), (6, 1), (6, 0), (7, 1), (7, 0), (5, 0), (8, 0), (4, 0), (3, 0), (2, 1),
     (2, 0), (1, 0),
 )
 GATES = (
-    ("R", 1), ("F", 2), ("S", 3), ("M", 2), ("N", 3), ("M", 3), None, ("M", 4), None, ("R", 2), ("R", 4), ("F", 3),
-    ("N", 4), ("N", 4), ("N", 4), ("S", 1),
+    ("S", 2), ("R", 2), None, None, ("R", 2), ("R", 2), ("F", 3), ("M", 1), ("R", 4), None, ("R", 2), ("F", 3),
+    None, ("F", 4), ("S", 3), ("S", 1),
 )
 DIRECT = (
     (0, 0), (1, 0), (1, 1), (2, 0), (2, 1), (3, 0), (3, 1), (4, 0), (4, 1), (8, 0),
 )
-RANK = {"A": 0, "M": 4, "R": 2, "S": 6, "F": 3, "N": 5, "Z": 3}
+RANK = {"A": 2, "M": 2, "R": 4, "S": 3, "F": 5, "N": 4, "Z": 1}
 
 
 class Plan:
@@ -288,21 +290,25 @@
         depth = WD.shape[0] * WD.shape[1]
         O[r, :] = jnp.dot(H[r, :], WD[...].reshape(depth, WD.shape[2]), preferred_element_type=F32)
 
+    def z_part(base, p):
+        rows, wide = B // D_ROWS, O.shape[1] // D_COLS
+        return pl.ds(base + p // D_COLS * rows, rows), pl.ds(p % D_COLS * wide, wide)
+
     def z_place(s, way, p):
-        size = B // D_PIECES
-        r = pl.ds(s * B + p * size, size)
-        return (YS.at[way, r], YR.at[way, r]) if s < WIDE_HOPS else (ZS.at[way, r], ZR.at[way, r])
+        r, c = z_part(s * B, p)
+        return (YS.at[way, r, c], YR.at[way, r, c]) if s < WIDE_HOPS else (ZS.at[way, r, c], ZR.at[way, r, c])
 
     def op_z(s, way, p):
-        rows = B // D_PIECES
-        total = O[pl.ds(plan.off((s, 1 - way if 0 < s < S else 0)) + p * rows, rows), :]
+        r, c = z_part(plan.off((s, 1 - way if 0 < s < S else 0)), p)
+        total = O[r, c]
         for v in (0, 1) if s == 0 else (way,):
             if s < S and p in plan.pieces(s + 1, v, D_PIECES):
                 got = z_place(s, v, p)[1]
                 arrived(("z", s, v, p), got, zway[v])
                 total = total + got[...].astype(F32)
         if s == 0:
-            out[pl.ds(p * rows, rows), :] = total.astype(BF16)
+            r, c = z_part(0, p)
+            out[r, c] = total.astype(BF16)
             return
         src, dst = z_place(s - 1, way, p)
         src[...] = total.astype(src.dtype)
@@ -310,6 +316,10 @@
 
     run = {"A": op_a, "M": op_m, "R": op_r, "S": op_s, "F": op_f, "N": op_n, "Z": op_z}
     for (name, *at), _ in plan.schedule():
+        if name == "Z" and at[0] == 0:
+            for m in started[: -2 * D_PIECES]:
+                m.wait_send()
+            del started[: -2 * D_PIECES]
         run[name](*at)
     for m in started:
         m.wait_send()

time: 109 us -> 110 us (level)
  no operation moved by 1% of the time
where the time goes in v6:
time: 110 us; the launch traced here: 109 us
  Pallas kernels  108 us (98%)
    pallas_call x1, Pallas kernels, body(): pl.pallas_call(functools.partial(kernel, plan), out_shape=pltpu.VMEM((blo...  108 us

profile of v6, /device:TPU:40, one launch (start us, length us, event | category | flops | bytes accessed | tf_op | source)
XLA Modules:
  0.0 109.0 jit_solution(4355704815001221673)
XLA Ops:
  0.0 108.4 %shard_map.46 = bf16[64,1024]{1,0:T(8,128)(2,1)S(1)} custom-call(bf16[64,1024]{1,0:T(8,128)(2,1)} %tok.1, bf16[448,1024]{1,0:T(8,128)(2,1)} %bitcast.2, bf16[448,1024]{1,0:T(8,128)(2,1)} %bitcast.3, bf16[448,1024]{1,0:T(8,128)(2,1)} %wd.1), custom_call_target="tpu_custom_call" | custom-call | tf_op jit(solution)/shard_map/pallas_call | solution.py:342
  108.4 0.7 copy.6

commit v7 on v6

--- a/solution.py
+++ b/solution.py
@@ -11,26 +11,27 @@
 F32 = jnp.float32
 BF16 = jnp.bfloat16
 
+LATENCY = {"x": 3.0, "z": 2.6}
 A_ROWS = 4
 A_COLS = 2
 A_PIECES = A_ROWS * A_COLS
 D_ROWS = 4
-D_COLS = 2
+D_COLS = 1
 D_PIECES = D_ROWS * D_COLS
 WIDE_HOPS = 2
 
 SEQUENCE = (
-    (0, 0), (1, 1), (3, 1), (4, 1), (5, 1), (6, 1), (6, 0), (7, 1), (7, 0), (5, 0), (8, 0), (4, 0), (3, 0), (2, 1),
-    (2, 0), (1, 0),
+    (0, 0), (1, 1), (3, 1), (4, 1), (5, 0), (6, 0), (6, 1), (7, 0), (7, 1), (5, 1), (8, 0), (4, 0), (3, 0), (1, 0),
+    (2, 0), (2, 1),
 )
 GATES = (
-    ("S", 2), ("R", 2), None, None, ("R", 2), ("R", 2), ("F", 3), ("M", 1), ("R", 4), None, ("R", 2), ("F", 3),
-    None, ("F", 4), ("S", 3), ("S", 1),
+    ("R", 2), ("R", 1), ("S", 4), ("R", 3), ("F", 4), ("M", 3), ("R", 3), ("R", 4), ("M", 2), ("M", 2), ("R", 2),
+    ("F", 3), None, ("R", 4), ("F", 4), ("R", 3),
 )
 DIRECT = (
-    (0, 0), (1, 0), (1, 1), (2, 0), (2, 1), (3, 0), (3, 1), (4, 0), (4, 1), (8, 0),
+    (0, 0), (1, 1), (2, 0), (2, 1), (3, 0), (3, 1), (4, 0), (4, 1), (8, 0),
 )
-RANK = {"A": 2, "M": 2, "R": 4, "S": 3, "F": 5, "N": 4, "Z": 1}
+RANK = {"A": 3, "M": 6, "R": 4, "S": 4, "F": 6, "N": 5, "Z": 1}
 
 
 class Plan:
@@ -112,7 +113,7 @@
             out.append((("Z", 0, 0, p), [("N", (0, 0))], [("z", 0, 0, p), ("z", 0, 1, p)], [], 0.05))
         return out
 
-    def schedule(self, latency=2.6, start=4.0):
+    def schedule(self, start=4.0):
         ops = self.ops()
         left = [len(op[1]) + len(op[2]) for op in ops]
         ready, free, users = [0.0] * len(ops), {}, {}
@@ -141,7 +142,7 @@
             known = [(name, 0.0)]
             for key, link, length in sends:
                 free[link] = max(free.get(link, 0.0), now) + length
-                known.append((key, free[link] + latency))
+                known.append((key, free[link] + LATENCY[link[0]]))
             for key, at in known:
                 for i in users.get(key, ()):
                     left[i] -= 1

time: 110 us -> 109 us (level)
    pallas_call x1, Pallas kernels: 108 us -> 107 us  [body(): pl.pallas_call(functools.partial(kernel, plan), out_shape=pltpu.VMEM((blo...]
where the time goes in v7:
time: 109 us; the launch traced here: 107 us
  Pallas kernels  107 us (98%)
    pallas_call x1, Pallas kernels, body(): pl.pallas_call(functools.partial(kernel, plan), out_shape=pltpu.VMEM((blo...  107 us

profile of v7, /device:TPU:40, one launch (start us, length us, event | category | flops | bytes accessed | tf_op | source)
XLA Modules:
  0.0 107.3 jit_solution(15456760785624131033)
XLA Ops:
  0.0 106.7 %shard_map.46 = bf16[64,1024]{1,0:T(8,128)(2,1)S(1)} custom-call(bf16[64,1024]{1,0:T(8,128)(2,1)} %tok.1, bf16[448,1024]{1,0:T(8,128)(2,1)} %bitcast.2, bf16[448,1024]{1,0:T(8,128)(2,1)} %bitcast.3, bf16[448,1024]{1,0:T(8,128)(2,1)} %wd.1), custom_call_target="tpu_custom_call" | custom-call | tf_op jit(solution)/shard_map/pallas_call | solution.py:343
  106.7 0.7 copy.6
